TPU v7x, 32 devices: a whole 2x2x4 slice. The times are simulated.
32 devices in a mesh: grp: 2 (over y), exp: 4 (over z), tp: 4 (over x, core).
Axes of the slice: x: 2, y: 2, z: 4, core: 2. Of those that a mesh axis runs over, the one named last changes fastest.
Arguments:
- tokens: bfloat16 [128, 3584], P(('grp', 'exp'), 'tp'), parts along dimension 0, may hold values from -6 to 6
- gate_up_weight: bfloat16 [3584, 2, 18944], P('tp', None, 'exp'), may hold values from -0.09375 to 0.09375
- down_weight: bfloat16 [18944, 3584], P('exp', 'tp'), may hold values from -0.046875 to 0.046875
- adapter_in: bfloat16 [4, 3584, 16], P('exp', 'tp'), may hold values from -0.09375 to 0.09375
- adapter_out: bfloat16 [4, 16, 3584], P('exp', None, 'tp'), may hold values from -1.5 to 1.5
- expert_ids: int32 [128, 2], P(('grp', 'exp')), parts along dimension 0, may hold values from 0 to 3, all different within a row; in each aligned block of 16 rows (0 to 15, 16 to 31, ...) at most 16 rows name the same one
- route_weight: float32 [128, 2], P(('grp', 'exp')), parts along dimension 0, may hold values from 0.2 to 1
Outputs:
- mixed: bfloat16 [128, 3584], P(('grp', 'exp'), 'tp'), parts along dimension 0
There are 2 independent parts, one for each index of `grp`. A program takes and returns all parts, laid end to end along the dimension named above; an argument that names none is the same for every part. Nothing has to cross between parts.
Inputs may be any that keep to these rules, and one draw needn't show every extreme that they name: `expert_ids`: each row names 2 different experts. Among the 16 rows of one index of exp (aligned blocks of 16 rows) no expert is named by more than 16 rows, and in every draw some expert is named by exactly 16 rows of some block.
All inputs are finite; a program needn't handle non-finite values.
Results may differ from a plain program's by a relative error of at most 0.025.
Values may be sent and summed in bfloat16 or wider, within the bound.
No kernel may reach another device: no remote copies, remote signals or barrier semaphores. Data moves between devices by JAX's collectives and lax.ppermute only.
A program may use at most 64 MiB of HBM per device.

v0:
```python
import jax
import jax.numpy as jnp
from jax import lax
from jax.sharding import PartitionSpec as P


def local(tokens, gate_up_weight, down_weight, adapter_in, adapter_out, expert_ids, route_weight):
    exp_count = lax.axis_size("exp")
    own_rows, feat_width = tokens.shape
    all_tokens = lax.all_gather(tokens, "exp", axis=0, tiled=True)
    hidden_width = gate_up_weight.shape[2]
    pair_weight = gate_up_weight.reshape(feat_width, 2 * hidden_width)
    pair_share = lax.psum_scatter(
        jnp.dot(all_tokens, pair_weight, preferred_element_type=jnp.float32).astype(jnp.bfloat16),
        "tp",
        scatter_dimension=0,
        tiled=True,
    ).astype(jnp.float32)
    hidden_share = (
        jax.nn.silu(pair_share[:, :hidden_width]) * pair_share[:, hidden_width:]
    ).astype(jnp.bfloat16)
    hidden = lax.all_gather(hidden_share, "tp", axis=0, tiled=True)
    base_out = lax.psum_scatter(
        jnp.dot(hidden, down_weight, preferred_element_type=jnp.float32).astype(jnp.bfloat16),
        "exp",
        scatter_dimension=0,
        tiled=True,
    ).astype(jnp.float32)
    top_count = expert_ids.shape[1]
    expert_count = adapter_in.shape[0] * exp_count
    flat_ids = expert_ids.reshape(own_rows * top_count)
    flat_weight = route_weight.reshape(own_rows * top_count)
    expert_hits = (flat_ids[:, None] == jnp.arange(expert_count, dtype=jnp.int32)[None, :]).astype(
        jnp.int32
    )
    capacity = max(2, 2 * top_count * own_rows // expert_count)
    slot_index = jnp.sum((jnp.cumsum(expert_hits, axis=0) - expert_hits) * expert_hits, axis=1)
    slot_target = flat_ids * capacity + slot_index
    slot_hits = (
        slot_target[:, None] == jnp.arange(expert_count * capacity, dtype=jnp.int32)[None, :]
    )
    combine_matrix = jnp.sum(
        (slot_hits.astype(jnp.float32) * flat_weight[:, None]).reshape(
            own_rows, top_count, expert_count * capacity
        ),
        axis=1,
    )
    dispatch_matrix = slot_hits.T.astype(jnp.bfloat16)
    repeated = jnp.repeat(tokens, top_count, axis=0)
    outgoing = jnp.dot(dispatch_matrix, repeated, preferred_element_type=jnp.float32).astype(
        jnp.bfloat16
    )
    outgoing = outgoing.reshape(expert_count, capacity, feat_width)
    rank_partial = jnp.einsum(
        "scd,dr->scr",
        lax.all_to_all(outgoing, "exp", split_axis=0, concat_axis=0, tiled=True),
        adapter_in[0],
        preferred_element_type=jnp.float32,
    )
    rank_mid = lax.psum(rank_partial, "tp").astype(jnp.bfloat16)
    expert_out = jnp.einsum(
        "scr,rd->scd", rank_mid, adapter_out[0], preferred_element_type=jnp.float32
    ).astype(jnp.bfloat16)
    returned = lax.all_to_all(expert_out, "exp", split_axis=0, concat_axis=0, tiled=True)
    adapter_sum = jnp.dot(
        combine_matrix,
        returned.reshape(expert_count * capacity, feat_width).astype(jnp.float32),
        precision=lax.Precision.HIGHEST,
        preferred_element_type=jnp.float32,
    )
    return (base_out + adapter_sum).astype(jnp.bfloat16)


def solution(mesh):
    in_specs = (
        P(("grp", "exp"), "tp"),
        P("tp", None, "exp"),
        P("exp", "tp"),
        P("exp", "tp", None),
        P("exp", None, "tp"),
        P(("grp", "exp"), None),
        P(("grp", "exp"), None),
    )
    out_specs = P(("grp", "exp"), "tp")
    return jax.shard_map(local, mesh=mesh, in_specs=in_specs, out_specs=out_specs, check_vma=False)
```

profile of v0, /device:TPU:0, one launch (start us, length us, event | category | flops | bytes accessed | tf_op | source)
XLA Modules:
  0.0 105.8 jit_solution(269650311221717586)
XLA Ops:
  6.5 0.0 copy-start
  6.5 0.0 reduce-scatter.3.cloned.1.call-start
  6.5 15.4 %all_gather.6 = bf16[64,896]{1,0:T(8,128)(2,1)S(1)} all-gather(bf16[16,896]{1,0:T(8,128)(2,1)} %param.7), channel_id=1, replica_groups=mesh['grp'=2,'exp'=4,'tp'=4] {'exp'}, dimensions={0}, use_global_device_ids=true | all-gather | bytes 143360 | tf_op jit(solution)/shard_map/all_gather | solution.py:10
  22.0 9.7 %copy.22 = bf16[112,8,2,4736]{3,1,2,0:T(8,128)(2,1)S(1)} copy(bf16[112,8,2,4736]{3,2,1,0:T(2,128)(2,1)} %bitcast.22) | data formatting | bytes 33947648
  31.7 0.0 copy-start.3
  31.7 0.0 copy-start.1
  31.7 0.0 copy-start.2
  31.7 3.5 %convolution_convert_fusion = bf16[64,9472]{1,0:T(8,128)(2,1)} fusion(bf16[64,896]{1,0:T(8,128)(2,1)S(1)} %all_gather.6, bf16[896,9472]{1,0:T(8,128)(2,1)S(1)} %bitcast.21), kind=kOutput, calls=%fused_computation | convolution fusion | flops 1086930944 | bytes 18300928 | tf_op jit(solution)/shard_map/dot_general | solution.py:14
  35.2 0.0 reduce-scatter.3.cloned.1.call-update
  35.2 0.0 copy-done.3
  35.2 0.1 copy.20
  35.3 0.1 eq.35
  35.4 0.0 copy-done.1
  35.5 0.1 fusion.6
  35.5 0.1 reduce_window_sum.11
  35.6 0.2 select_reduce_fusion.1
  35.8 1.0 convolution_convert_fusion.2
  36.8 4.8 %all-to-all-start = ((bf16[4,16,896]{2,1,0:T(8,128)(2,1)}), bf16[4,16,896]{2,1,0:T(8,128)(2,1)S(1)}, u32[]{:S(2)}, u32[]{:S(2)}) async-start(bf16[4,16,896]{2,1,0:T(8,128)(2,1)} %bitcast), calls=%async_computation.2 | async-start | bytes 229376 | tf_op jit(solution)/shard_map/all_to_all | solution.py:56
  41.6 0.1 reduce_sum.21
  41.6 0.1 copy.21
  41.7 5.7 %all-to-all-done = bf16[4,16,896]{2,1,0:T(8,128)(2,1)S(1)} async-done(((bf16[4,16,896]{2,1,0:T(8,128)(2,1)}), bf16[4,16,896]{2,1,0:T(8,128)(2,1)S(1)}, u32[]{:S(2)}, u32[]{:S(2)}) %all-to-all-start) | async-done | bytes 114720 | tf_op jit(solution)/shard_map/all_to_all | solution.py:56
  47.4 0.0 copy-done.2
  47.4 0.2 fusion.3
  47.6 11.2 %psum.7 = bf16[4,16,16]{2,1,0:T(8,128)(2,1)S(1)} all-reduce(f32[4,16,16]{2,1,0:T(8,128)S(1)} %fusion.3), channel_id=1, replica_groups=mesh['grp'=2,'exp'=4,'tp'=4] {'tp'}, use_global_device_ids=true, to_apply=%region_5.6 | all-reduce | flops 1024 | bytes 6144 | tf_op jit(solution)/shard_map/psum | solution.py:60
  58.8 0.0 copy-done
  58.8 0.8 convolution_convert_fusion.1
  59.6 3.3 %all-to-all-start.1 = ((bf16[4,16,896]{2,1,0:T(8,128)(2,1)}), bf16[4,16,896]{2,1,0:T(8,128)(2,1)S(1)}, u32[]{:S(2)}, u32[]{:S(2)}) async-start(bf16[4,16,896]{2,1,0:T(8,128)(2,1)} %convolution_convert_fusion.1), calls=%async_computation.3 | async-start | bytes 229376 | tf_op jit(solution)/shard_map/all_to_all | solution.py:64
  62.9 0.0 reduce-scatter.5.cloned.1.call-start
  63.0 0.0 reduce-scatter.3.cloned.1.call-done
  63.0 1.0 convert_element_type.34
  64.0 0.1 fusion.1
  64.1 7.7 %all_gather.7 = bf16[64,4736]{1,0:T(8,128)(2,1)S(1)} all-gather(bf16[16,4736]{1,0:T(8,128)(2,1)S(1)} %fusion.1), channel_id=1, replica_groups=mesh['grp'=2,'exp'=4,'tp'=4] {'tp'}, dimensions={0}, use_global_device_ids=true | all-gather | bytes 757760 | tf_op jit(solution)/shard_map/all_gather | solution.py:22
  71.8 0.0 copy-start.4
  71.8 5.5 %convolution_convert_fusion.3 = bf16[64,896]{1,0:T(8,128)(2,1)} fusion(bf16[64,4736]{1,0:T(8,128)(2,1)S(1)} %all_gather.7, bf16[4736,896]{1,0:T(8,128)(2,1)} %param.9), kind=kOutput, calls=%fused_computation.3 | convolution fusion | flops 543219712 | bytes 9207808 | tf_op jit(solution)/shard_map/dot_general | solution.py:24
  77.3 0.0 reduce-scatter.5.cloned.1.call-update
  77.3 0.0 copy-done.4
  77.3 0.1 select_reduce_fusion
  77.4 0.0 all-to-all-done.1
  77.4 20.0 %reduce-scatter.5.cloned.1.call-done = bf16[16,896]{1,0:T(8,128)(2,1)} async-done(((bf16[64,896]{1,0:T(8,128)(2,1)}), bf16[16,896]{1,0:T(8,128)(2,1)}) %reduce-scatter.5.cloned.1.call-update) | async-done | bytes 28688 | tf_op jit(solution)/shard_map/reduce_scatter | solution.py:23
  97.4 1.5 %fusion = bf16[16,896]{1,0:T(8,128)(2,1)} fusion(f32[16,64]{1,0:T(8,128)S(1)} %select_reduce_fusion, bf16[64,896]{1,0:T(8,128)(2,1)S(1)} %bitcast.23, bf16[16,896]{1,0:T(8,128)(2,1)} %reduce-scatter.5.cloned.1.call-done), kind=kOutput, calls=%fused_computation.5 | convolution fusion | flops 11053056 | bytes 176128 | tf_op jit(solution)/shard_map/dot_general | solution.py:65
  (4 shorter events, 0.1 us)
Async XLA Ops:
  6.5 52.3 %copy-start = (bf16[1,16,896]{2,1,0:T(8,128)(2,1)S(1)}, bf16[1,16,896]{2,1,0:T(8,128)(2,1)}, u32[]{:S(2)}) copy-start(bf16[1,16,896]{2,1,0:T(8,128)(2,1)} %param.11) | copy-start | bytes 86020
  6.5 56.4 %reduce-scatter.3.cloned.1.call-start = ((), (), s32[]{:S(2)}) async-start(), calls=%async_computation.4 | async-start | bytes 1515520 | tf_op jit(solution)/shard_map/reduce_scatter | solution.py:13
  31.7 3.5 %copy-start.3 = (s32[16,2]{0,1:T(2,128)S(1)}, s32[16,2]{0,1:T(2,128)}, u32[]{:S(2)}) copy-start(s32[16,2]{0,1:T(2,128)} %param.12) | copy-start | bytes 388
  31.7 3.7 %copy-start.1 = (bf16[16,896]{1,0:T(8,128)(2,1)S(1)}, bf16[16,896]{1,0:T(8,128)(2,1)}, u32[]{:S(2)}) copy-start(bf16[16,896]{1,0:T(8,128)(2,1)} %param.7) | copy-start | bytes 86020
  31.7 15.7 %copy-start.2 = (bf16[1,896,16]{1,2,0:T(8,128)(2,1)S(1)}, bf16[1,896,16]{1,2,0:T(8,128)(2,1)}, u32[]{:S(2)}) copy-start(bf16[1,896,16]{1,2,0:T(8,128)(2,1)} %param.10) | copy-start | bytes 86020
  36.8 10.7 %all-to-all-start = ((bf16[4,16,896]{2,1,0:T(8,128)(2,1)}), bf16[4,16,896]{2,1,0:T(8,128)(2,1)S(1)}, u32[]{:S(2)}, u32[]{:S(2)}) async-start(bf16[4,16,896]{2,1,0:T(8,128)(2,1)} %bitcast), calls=%async_computation.2 | async-start | bytes 229376 | tf_op jit(solution)/shard_map/all_to_all | solution.py:56
  59.6 17.8 %all-to-all-start.1 = ((bf16[4,16,896]{2,1,0:T(8,128)(2,1)}), bf16[4,16,896]{2,1,0:T(8,128)(2,1)S(1)}, u32[]{:S(2)}, u32[]{:S(2)}) async-start(bf16[4,16,896]{2,1,0:T(8,128)(2,1)} %convolution_convert_fusion.1), calls=%async_computation.3 | async-start | bytes 229376 | tf_op jit(solution)/shard_map/all_to_all | solution.py:64
  62.9 34.5 %reduce-scatter.5.cloned.1.call-start = ((), (), s32[]{:S(2)}) async-start(), calls=%async_computation.5 | async-start | bytes 143360 | tf_op jit(solution)/shard_map/reduce_scatter | solution.py:23
  71.8 5.5 %copy-start.4 = (f32[16,2]{0,1:T(2,128)S(1)}, f32[16,2]{0,1:T(2,128)}, u32[]{:S(2)}) copy-start(f32[16,2]{0,1:T(2,128)} %param.13) | copy-start | bytes 388
Sparse Core Ops, SparseCore 0:
  35.3 27.2 reduce-scatter.2
  77.4 19.9 reduce-scatter.4
where the time goes:
time: 106 us
  blocking collectives  34.4 us (32%)
  waiting for transfers between devices  25.7 us (24%)
  between operations  13.5 us (13%)
  matrix products  12.4 us (12%)
  local copies, waits for them, and re-layouts  10.1 us (10%)
  starting transfers between devices  8.16 us (8%)
  other arithmetic  1.49 us (1%)
    reduce_scatter x1, waiting for transfers between devices, local(): lax.psum_scatter(jnp.dot(hidden, down_weight, preferred_element_type=jnp....  20 us
    all_gather x1, blocking collectives, local(): all_tokens = lax.all_gather(tokens, 'exp', axis=0, tiled=True)  15.4 us
    psum x1, blocking collectives, local(): rank_mid = lax.psum(rank_partial, 'tp').astype(jnp.bfloat16)  11.2 us
    unnamed x12, local copies, waits for them, and re-layouts  9.81 us
    all_gather x1, blocking collectives, local(): hidden = lax.all_gather(hidden_share, 'tp', axis=0, tiled=True)  7.73 us
    all_to_all x1, waiting for transfers between devices, local(): lax.all_to_all(outgoing, 'exp', split_axis=0, concat_axis=0, tiled=True)  5.71 us
    dot_general x1, matrix products, local(): jnp.dot(hidden, down_weight, preferred_element_type=jnp.float32)  5.47 us
    all_to_all x1, starting transfers between devices, local(): lax.all_to_all(outgoing, 'exp', split_axis=0, concat_axis=0, tiled=True)  4.8 us
  transfers between devices with their start and end apart: 4, of which 2 were waited for; matrix products, arithmetic and copies ran while one was open for 9% of the time, Pallas kernels for 0%

commit v1 on v0

--- a/solution.py
+++ b/solution.py
@@ -1,10 +1,248 @@
+import functools
+
 import jax
 import jax.numpy as jnp
 from jax import lax
+from jax.experimental import pallas as pl
+from jax.experimental.pallas import tpu as pltpu
 from jax.sharding import PartitionSpec as P
 
-
-def local(tokens, gate_up_weight, down_weight, adapter_in, adapter_out, expert_ids, route_weight):
+LANES = 128
+BF16 = jnp.bfloat16
+F32 = jnp.float32
+VM = pl.BlockSpec(memory_space=pltpu.VMEM)
+HBM = pl.BlockSpec(memory_space=pltpu.HBM)
+FLIP = (0, 2, 1, 3)
+
+
+def in_hbm(x):
+    return pltpu.with_memory_space_constraint(x, pltpu.HBM)
+
+
+def params(mib):
+    return pltpu.CompilerParams(vmem_limit_bytes=mib * 2**20)
+
+
+def tile_copies(weight_ref, tiles_ref, sems, first):
+    rows = 2 * weight_ref.shape[0]
+    flat = weight_ref.reshape(rows, weight_ref.shape[2])
+    return [
+        pltpu.make_async_copy(
+            flat.at[:, pl.ds((first + j) * LANES, LANES)], tiles_ref.at[j], sems.at[j]
+        )
+        for j in range(tiles_ref.shape[0])
+    ]
+
+
+def prep_kernel(
+    tokens_in, ids_in, route_in, weight_ref, ext_ref, tiles_ref,
+    tokens_ref, ids_ref, route_ref, own_sems, sems, *, first
+):
+    small = [
+        pltpu.make_async_copy(source, target, own_sems.at[i])
+        for i, (source, target) in enumerate(
+            ((tokens_in, tokens_ref), (ids_in, ids_ref), (route_in, route_ref))
+        )
+    ]
+    copies = tile_copies(weight_ref, tiles_ref, sems, first)
+    for copy in small + copies:
+        copy.start()
+    for copy in small:
+        copy.wait()
+    top, rows = ids_ref.shape
+    feat = tokens_ref.shape[1]
+    number = lax.broadcasted_iota(jnp.int32, (LANES // 2, rows), 0)
+    coef = jnp.zeros((LANES // 2, rows), F32)
+    for k in range(top):
+        coef = coef + jnp.where(ids_ref[k : k + 1, :] == number, route_ref[k : k + 1, :], 0.0)
+    high = coef.astype(BF16)
+    low = (coef - high.astype(F32)).astype(BF16)
+    both = jnp.concatenate([high.astype(F32), low.astype(F32)], axis=0).astype(BF16)
+    eye = (
+        lax.broadcasted_iota(jnp.int32, (rows, rows), 0)
+        == lax.broadcasted_iota(jnp.int32, (rows, rows), 1)
+    ).astype(F32).astype(BF16)
+    turned = lax.dot_general(eye, both, (((1,), (1,)), ((), ())), preferred_element_type=F32)
+    ext_ref[:, :feat] = tokens_ref[...]
+    ext_ref[:, feat:] = turned.astype(BF16)
+    for copy in copies:
+        copy.wait()
+
+
+def load_kernel(weight_ref, tiles_ref, sems, *, first):
+    copies = tile_copies(weight_ref, tiles_ref, sems, first)
+    for copy in copies:
+        copy.start()
+    for copy in copies:
+        copy.wait()
+
+
+def pair_kernel(*refs, parts, feat):
+    x_refs, refs = refs[:4], refs[4:]
+    tile_refs, refs = refs[:parts], refs[parts:]
+    in_ref, keep_ref, send_ref, all_ref, wide_ref = refs
+    own = lax.axis_index("tp")
+    rows = x_refs[0].shape[0]
+    for s in range(4):
+        all_ref[s] = x_refs[s][:, :feat]
+    x = jnp.concatenate([all_ref[own ^ FLIP[i]] for i in range(4)], axis=0)
+    half = 2 * rows
+    rank = lax.dot_general(x, in_ref[...], (((1,), (1,)), ((), ())), preferred_element_type=F32)
+    rank = jnp.concatenate([rank, jnp.zeros((4 * rows, LANES - rank.shape[1]), F32)], axis=1)
+    spread = (
+        2 * lax.broadcasted_iota(jnp.int32, (LANES, 2 * LANES), 0)
+        == lax.broadcasted_iota(jnp.int32, (LANES, 2 * LANES), 1)
+    ).astype(F32).astype(BF16)
+    for b in range(feat // LANES):
+        gate = jnp.dot(x[:, b * LANES : (b + 1) * LANES], spread, preferred_element_type=F32)
+        up = pltpu.roll(gate, 1, 1).astype(BF16)
+        gate = gate.astype(BF16)
+        at = slice(2 * b * LANES, 2 * (b + 1) * LANES)
+        wide_ref[0:half, at] = gate[:half]
+        wide_ref[half : 2 * half, at] = up[:half]
+        wide_ref[2 * half : 3 * half, at] = gate[half:]
+        wide_ref[3 * half : 4 * half, at] = up[half:]
+    width = (keep_ref.shape[1] - LANES) // 2
+    keep_ref[:, 2 * width :] = rank[:half]
+    send_ref[:, 2 * width :] = rank[half:].astype(BF16)
+    at = 0
+    for tiles_ref in tile_refs:
+        count = tiles_ref.shape[0]
+        for j in range(0, count, 2):
+            n = min(2, count - j)
+            weight = tiles_ref[j]
+            if n == 2:
+                weight = jnp.concatenate([weight, tiles_ref[j + 1]], axis=1)
+            acc = jnp.dot(wide_ref[...], weight, preferred_element_type=F32)
+            cols = slice(at, at + n * LANES)
+            more = slice(width + at, width + at + n * LANES)
+            keep_ref[:, cols] = acc[:half]
+            keep_ref[:, more] = acc[half : 2 * half]
+            send_ref[:, cols] = acc[2 * half : 3 * half].astype(BF16)
+            send_ref[:, more] = acc[3 * half :].astype(BF16)
+            at += n * LANES
+
+
+def add_kernel(keep_ref, got_ref, mine_ref, send_ref):
+    rows = mine_ref.shape[0]
+    mine_ref[...] = keep_ref[:rows] + got_ref[:rows].astype(F32)
+    send_ref[...] = (keep_ref[rows:] + got_ref[rows:].astype(F32)).astype(BF16)
+
+
+def gate_kernel(mine_ref, got_ref, hidden_ref):
+    width = (mine_ref.shape[1] - LANES) // 2
+    gate = mine_ref[:, :width] + got_ref[:, :width].astype(F32)
+    up = mine_ref[:, width : 2 * width] + got_ref[:, width : 2 * width].astype(F32)
+    hidden_ref[:, :width] = (gate / (1.0 + jnp.exp(-gate)) * up).astype(BF16)
+    hidden_ref[:, width:] = (mine_ref[:, 2 * width :] + got_ref[:, 2 * width :].astype(F32)).astype(BF16)
+
+
+def down_kernel(*refs, feat, rank):
+    h_refs, x_refs, (weight_ref, out_map_ref), o_refs, (turn_ref, all_ref) = (
+        refs[:4], refs[4:8], refs[8:10], refs[10:14], refs[14:]
+    )
+    own = lax.axis_index("tp")
+    expert = lax.axis_index("exp")
+    rows = h_refs[0].shape[0]
+    width = weight_ref.shape[0]
+    for s in range(4):
+        all_ref[s] = x_refs[s][:, feat:]
+    hidden = jnp.concatenate([h[...] for h in h_refs], axis=0)
+    acc = jnp.dot(hidden[:, :width], weight_ref[...], preferred_element_type=F32)
+    lifted = jnp.dot(hidden[:, width : width + rank], out_map_ref[...], preferred_element_type=F32)
+    lifted = lifted.astype(BF16).astype(F32)
+    lane = lax.broadcasted_iota(jnp.int32, (4 * rows, LANES), 1)
+    coef = jnp.concatenate([all_ref[own ^ FLIP[i]] for i in range(4)], axis=0).astype(F32)
+    mine = (lane == expert) | (lane == expert + LANES // 2)
+    coef = jnp.sum(jnp.where(mine, coef, 0.0), axis=1, keepdims=True)
+    acc = acc + coef * lifted
+    for i in range(4):
+        turn_ref[own ^ FLIP[i]] = acc[i * rows : (i + 1) * rows]
+    o_refs[0][...] = turn_ref[0]
+    for s in range(1, 4):
+        o_refs[s][...] = turn_ref[s].astype(BF16)
+
+
+def swap(x, bit):
+    return lax.ppermute(x, "tp", [(t, t ^ bit) for t in range(4)])
+
+
+def fast(tokens, gate_up_weight, down_weight, adapter_in, adapter_out, expert_ids, route_weight):
+    rows, feat = tokens.shape
+    width = gate_up_weight.shape[2]
+    rank = adapter_in.shape[2]
+    count = width // LANES
+    first = count // 2
+    tiles = lambda n: pltpu.VMEM((n, 2 * feat, LANES), BF16)
+    ext, tiles_a = pl.pallas_call(
+        functools.partial(prep_kernel, first=0),
+        out_shape=(jax.ShapeDtypeStruct((rows, feat + LANES), BF16), tiles(first)),
+        in_specs=[HBM] * 4,
+        out_specs=(VM, VM),
+        scratch_shapes=[
+            pltpu.VMEM((rows, feat), BF16),
+            pltpu.VMEM(expert_ids.shape[::-1], jnp.int32),
+            pltpu.VMEM(route_weight.shape[::-1], F32),
+            pltpu.SemaphoreType.DMA((3,)),
+            pltpu.SemaphoreType.DMA((first,)),
+        ],
+        compiler_params=params(2),
+    )(*(in_hbm(a) for a in (tokens, expert_ids.T, route_weight.T, gate_up_weight)))
+    xs = [ext] + [
+        lax.ppermute(ext, "exp", [(e, (e + s) % 4) for e in range(4)]) for s in range(1, 4)
+    ]
+    tiles_b = pl.pallas_call(
+        functools.partial(load_kernel, first=first),
+        out_shape=tiles(count - first),
+        in_specs=[HBM],
+        out_specs=VM,
+        scratch_shapes=[pltpu.SemaphoreType.DMA((count - first,))],
+        compiler_params=params(2),
+    )(in_hbm(gate_up_weight))
+    total = 2 * width + LANES
+    shape = jax.ShapeDtypeStruct
+    keep, send = pl.pallas_call(
+        functools.partial(pair_kernel, parts=2, feat=feat),
+        out_shape=(shape((2 * rows, total), F32), shape((2 * rows, total), BF16)),
+        in_specs=[VM] * 7,
+        out_specs=(VM, VM),
+        scratch_shapes=[pltpu.VMEM((4, rows, feat), BF16), pltpu.VMEM((8 * rows, 2 * feat), BF16)],
+        compiler_params=params(8),
+    )(*xs, tiles_a, tiles_b, jnp.swapaxes(adapter_in, 1, 2)[0])
+    got = swap(send, 1)
+    mine, send = pl.pallas_call(
+        add_kernel,
+        out_shape=(shape((rows, total), F32), shape((rows, total), BF16)),
+        in_specs=[VM, VM],
+        out_specs=(VM, VM),
+        compiler_params=params(4),
+    )(keep, got)
+    got = swap(send, 2)
+    hidden = pl.pallas_call(
+        gate_kernel,
+        out_shape=shape((rows, width + LANES), BF16),
+        in_specs=[VM, VM],
+        out_specs=VM,
+        compiler_params=params(4),
+    )(mine, got)
+    far = swap(hidden, 2)
+    hs = [hidden, far, swap(hidden, 1), swap(far, 1)]
+    outs = pl.pallas_call(
+        functools.partial(down_kernel, feat=feat, rank=rank),
+        out_shape=[shape((rows, feat), F32)] + [shape((rows, feat), BF16)] * 3,
+        in_specs=[VM] * 10,
+        out_specs=[VM] * 4,
+        scratch_shapes=[pltpu.VMEM((4, rows, feat), F32), pltpu.VMEM((4, rows, LANES), BF16)],
+        compiler_params=params(16),
+    )(*hs, *xs, down_weight, adapter_out[0])
+    total = outs[0]
+    for s in range(1, 4):
+        back = lax.ppermute(outs[s], "exp", [(e, (e - s) % 4) for e in range(4)])
+        total = total + back.astype(F32)
+    return total.astype(BF16)
+
+
+def plain(tokens, gate_up_weight, down_weight, adapter_in, adapter_out, expert_ids, route_weight):
     exp_count = lax.axis_size("exp")
     own_rows, feat_width = tokens.shape
     all_tokens = lax.all_gather(tokens, "exp", axis=0, tiled=True)
@@ -82,4 +320,12 @@
         P(("grp", "exp"), None),
     )
     out_specs = P(("grp", "exp"), "tp")
+    def local(*args):
+        rows, feat = args[0].shape
+        width = args[1].shape[2]
+        aligned = feat % LANES == 0 and width % LANES == 0 and rows % 16 == 0
+        few = args[3].shape[0] == 1 and mesh.shape["exp"] <= LANES // 2
+        square = mesh.shape["tp"] == 4 and mesh.shape["exp"] == 4
+        return (fast if aligned and few and square else plain)(*args)
+
     return jax.shard_map(local, mesh=mesh, in_specs=in_specs, out_specs=out_specs, check_vma=False)

time: 106 us -> 47 us (0.44)
  blocking collectives: 34.4 us -> 0 us
  between operations: 13.5 us -> 0.11 us
  matrix products: 12.4 us -> 0 us
  Pallas kernels: 0 us -> 12.1 us
  local copies, waits for them, and re-layouts: 10.1 us -> 0.02 us
  starting transfers between devices: 8.16 us -> 12.7 us
  waiting for transfers between devices: 25.7 us -> 21.4 us
    all_gather x2 -> x0, blocking collectives: 23.2 us -> none  [the longest x1 15.4 us: local(): all_tokens = lax.all_gather(tokens, 'exp', axis=0, tiled=True)]
    ppermute x0 -> x11, waiting for transfers between devices: none -> 21.4 us  [the longest x5 14.9 us: swap(): return lax.ppermute(x, 'tp', [(t, t ^ bit) for t in range(4)])]
    reduce_scatter x2 -> x0, waiting for transfers between devices: 20 us -> none  [the longest x1 20 us: local(): lax.psum_scatter(jnp.dot(hidden, down_weight, preferred_element_type=jnp....]
    ppermute x0 -> x11, starting transfers between devices: none -> 12.7 us  [the longest x3 6.14 us: fast(): lax.ppermute(ext, 'exp', [(e, (e + s) % 4) for e in range(4)])]
    dot_general x6 -> x0, matrix products: 12.4 us -> none  [the longest x1 5.47 us: local(): jnp.dot(hidden, down_weight, preferred_element_type=jnp.float32)]
    pallas_call x0 -> x6, Pallas kernels: none -> 12.1 us  [the longest x1 3.92 us: fast(): pl.pallas_call(functools.partial(load_kernel, first=first), out_shape=til...]
    psum x1 -> x0, blocking collectives: 11.2 us -> none  [local(): rank_mid = lax.psum(rank_partial, 'tp').astype(jnp.bfloat16)]
    unnamed x12 -> x10, local copies, waits for them, and re-layouts: 9.81 us -> 0.02 us
  transfers between devices with their start and end apart: 4 -> 11, of which waited for: 2 -> 8; matrix products, arithmetic and copies ran while one was open for 9% -> 0% of each run, Pallas kernels for 0% -> 8%
where the time goes in v1:
time: 47 us; the launch traced here: 46.9 us
  waiting for transfers between devices  21.4 us (46%)
  starting transfers between devices  12.7 us (27%)
  Pallas kernels  12.1 us (26%)
  other arithmetic  0.63 us (1%)
    ppermute x5, waiting for transfers between devices, swap(): return lax.ppermute(x, 'tp', [(t, t ^ bit) for t in range(4)])  14.9 us
    ppermute x3, starting transfers between devices, fast(): lax.ppermute(ext, 'exp', [(e, (e + s) % 4) for e in range(4)])  6.14 us
    ppermute x3, waiting for transfers between devices, fast(): back = lax.ppermute(outs[s], 'exp', [(e, (e - s) % 4) for e in range(4)])  5.66 us
    pallas_call x1, Pallas kernels, fast(): pl.pallas_call(functools.partial(load_kernel, first=first), out_shape=til...  3.92 us
    pallas_call x1, Pallas kernels, fast(): pl.pallas_call(functools.partial(prep_kernel, first=0), out_shape=(jax.Sh...  3.81 us
    ppermute x3, starting transfers between devices, fast(): back = lax.ppermute(outs[s], 'exp', [(e, (e - s) % 4) for e in range(4)])  3.3 us
    ppermute x5, starting transfers between devices, swap(): return lax.ppermute(x, 'tp', [(t, t ^ bit) for t in range(4)])  3.2 us
    pallas_call x1, Pallas kernels, fast(): pl.pallas_call(functools.partial(pair_kernel, parts=2, feat=feat), out_sh...  2.64 us
  transfers between devices with their start and end apart: 11, of which 8 were waited for; matrix products, arithmetic and copies ran while one was open for 0% of the time, Pallas kernels for 8%

profile of v1, /device:TPU:0, one launch (start us, length us, event | category | flops | bytes accessed | tf_op | source)
XLA Modules:
  0.0 46.9 jit_solution(12680725028794027164)
XLA Ops:
  0.0 3.8 %shard_map.73 = (bf16[16,1024]{1,0:T(8,128)(2,1)S(1)}, bf16[18,1792,128]{2,1,0:T(8,128)(2,1)S(1)}) custom-call(bf16[16,896]{1,0:T(8,128)(2,1)} %tokens_in.1, s32[2,16]{1,0:T(2,128)} %bitcast.10, f32[2,16]{1,0:T(2,128)} %bitcast.11, bf16[896,2,4736]{2,1,0:T(2,128)(2,1)} %weight_ref.3), custom_call_target="tpu_custom_call" | custom-call | tf_op jit(solution)/shard_map/pallas_call | solution.py:177
  3.8 0.0 copy-start
  3.8 5.1 %collective-permute-start.2 = (bf16[16,1024]{1,0:T(8,128)(2,1)S(1)}, bf16[16,1024]{1,0:T(8,128)(2,1)S(1)}, u32[]{:S(2)}, u32[]{:S(2)}) collective-permute-start(bf16[16,1024]{1,0:T(8,128)(2,1)S(1)} %get-tuple-element.15.refs_0_.refs_4_), channel_id=1, source_target_pairs={{0,12},{4,0},{8,4},{12,8},{1,13},{5,1},{9,5},{13,9},{2,14},{6,2},{... | collective-permute-start | bytes 98312 | tf_op jit(solution)/shard_map/ppermute | solution.py:192
  9.0 0.0 collective-permute-start.1
  9.0 1.0 %collective-permute-start = (bf16[16,1024]{1,0:T(8,128)(2,1)S(1)}, bf16[16,1024]{1,0:T(8,128)(2,1)S(1)}, u32[]{:S(2)}, u32[]{:S(2)}) collective-permute-start(bf16[16,1024]{1,0:T(8,128)(2,1)S(1)} %get-tuple-element.15.refs_0_.refs_4_), channel_id=1, source_target_pairs={{0,4},{4,8},{8,12},{12,0},{1,5},{5,9},{9,13},{13,1},{2,6},{6,10},{... | collective-permute-start | bytes 98312 | tf_op jit(solution)/shard_map/ppermute | solution.py:192
  10.0 3.9 %shard_map.74.refs_5_ = bf16[19,1792,128]{2,1,0:T(8,128)(2,1)S(1)} custom-call(bf16[896,2,4736]{2,1,0:T(2,128)(2,1)} %weight_ref.3), custom_call_target="tpu_custom_call" | custom-call | tf_op jit(solution)/shard_map/pallas_call | solution.py:194
  13.9 0.0 collective-permute-done.2.refs_3_.refs_7_
  13.9 0.0 collective-permute-done.1.refs_2_.refs_6_
  13.9 0.7 %collective-permute-done.refs_1_.refs_5_ = bf16[16,1024]{1,0:T(8,128)(2,1)S(1)} collective-permute-done((bf16[16,1024]{1,0:T(8,128)(2,1)S(1)}, bf16[16,1024]{1,0:T(8,128)(2,1)S(1)}, u32[]{:S(2)}, u32[]{:S(2)}) %collective-permute-start) | collective-permute-done | bytes 32800 | tf_op jit(solution)/shard_map/ppermute | solution.py:192
  14.7 0.0 slice-start
  14.7 0.0 copy-done
  14.7 0.0 slice-start.1
  14.7 0.0 slice-start.2
  14.7 0.0 copy-start.1
  14.7 2.6 %shard_map.75 = (f32[32,9600]{1,0:T(8,128)S(1)}, bf16[32,9600]{1,0:T(8,128)(2,1)S(1)}) custom-call(bf16[16,1024]{1,0:T(8,128)(2,1)S(1)} %get-tuple-element.15.refs_0_.refs_4_, bf16[16,1024]{1,0:T(8,128)(2,1)S(1)} %collective-permute-done.refs_1_.refs_5_, bf16[16,1024]{1,0:T(8,128)(2,1)S(1)} %collective-permute-done.1.refs_2_.refs_6_, ...), custom_call_target="tpu_custom_call" | custom-call | tf_op jit(solution)/shard_map/pallas_call | solution.py:204
  17.4 0.1 collective-permute-start.3
  17.4 2.0 %collective-permute-done.3.got_ref = bf16[32,9600]{1,0:T(8,128)(2,1)S(1)} collective-permute-done((bf16[32,9600]{1,0:T(8,128)(2,1)S(1)}, bf16[32,9600]{1,0:T(8,128)(2,1)S(1)}, u32[]{:S(2)}, u32[]{:S(2)}) %collective-permute-start.3) | collective-permute-done | bytes 614432 | tf_op jit(solution)/shard_map/ppermute | solution.py:167
  19.5 0.1 shard_map.76
  19.6 1.6 %collective-permute-start.4 = (bf16[16,9600]{1,0:T(8,128)(2,1)S(1)}, bf16[16,9600]{1,0:T(8,128)(2,1)S(1)}, u32[]{:S(2)}, u32[]{:S(2)}) collective-permute-start(bf16[16,9600]{1,0:T(8,128)(2,1)S(1)} %get-tuple-element.20), channel_id=1, source_target_pairs={{0,2},{1,3},{2,0},{3,1},{4,6},{5,7},{6,4},{7,5},{8,10},{9,11},{10,... | collective-permute-start | bytes 921608 | tf_op jit(solution)/shard_map/ppermute | solution.py:167
  21.1 7.8 %collective-permute-done.4.got_ref = bf16[16,9600]{1,0:T(8,128)(2,1)S(1)} collective-permute-done((bf16[16,9600]{1,0:T(8,128)(2,1)S(1)}, bf16[16,9600]{1,0:T(8,128)(2,1)S(1)}, u32[]{:S(2)}, u32[]{:S(2)}) %collective-permute-start.4) | collective-permute-done | bytes 307232 | tf_op jit(solution)/shard_map/ppermute | solution.py:167
  28.9 0.1 shard_map.77.refs_0_
  29.1 1.6 %collective-permute-start.5 = (bf16[16,4864]{1,0:T(8,128)(2,1)S(1)}, bf16[16,4864]{1,0:T(8,128)(2,1)S(1)}, u32[]{:S(2)}, u32[]{:S(2)}) collective-permute-start(bf16[16,4864]{1,0:T(8,128)(2,1)S(1)} %shard_map.77.refs_0_), channel_id=1, source_target_pairs={{0,2},{1,3},{2,0},{3,1},{4,6},{5,7},{6,4},{7,5},{8,10},{9,11},{10,... | collective-permute-start | bytes 466952 | tf_op jit(solution)/shard_map/ppermute | solution.py:167
  30.6 0.0 collective-permute-start.6
  30.6 3.7 %collective-permute-done.5.refs_1_ = bf16[16,4864]{1,0:T(8,128)(2,1)S(1)} collective-permute-done((bf16[16,4864]{1,0:T(8,128)(2,1)S(1)}, bf16[16,4864]{1,0:T(8,128)(2,1)S(1)}, u32[]{:S(2)}, u32[]{:S(2)}) %collective-permute-start.5) | collective-permute-done | bytes 155680 | tf_op jit(solution)/shard_map/ppermute | solution.py:167
  34.4 0.0 collective-permute-start.7
  34.4 0.0 collective-permute-done.6.refs_2_
  34.4 1.4 %collective-permute-done.7.refs_3_ = bf16[16,4864]{1,0:T(8,128)(2,1)S(1)} collective-permute-done((bf16[16,4864]{1,0:T(8,128)(2,1)S(1)}, bf16[16,4864]{1,0:T(8,128)(2,1)S(1)}, u32[]{:S(2)}, u32[]{:S(2)}) %collective-permute-start.7) | collective-permute-done | bytes 155680 | tf_op jit(solution)/shard_map/ppermute | solution.py:167
  35.8 0.0 slice-done
  35.8 0.0 slice-done.1
  35.8 0.0 slice-done.2
  35.8 0.0 copy-done.1
  35.8 1.5 %shard_map.78 = (f32[16,896]{1,0:T(8,128)S(1)}, bf16[16,896]{1,0:T(8,128)(2,1)S(1)}, bf16[16,896]{1,0:T(8,128)(2,1)S(1)}, bf16[16,896]{1,0:T(8,128)(2,1)S(1)}) custom-call(bf16[16,4864]{1,0:T(8,128)(2,1)S(1)} %shard_map.77.refs_0_, bf16[16,4864]{1,0:T(8,128)(2,1)S(1)} %collective-permute-done.5.refs_1_, bf16[16,4864]{1,0:T(8,128)(2,1)S(1)} %collective-permute-done.6.refs_2_, ...), custom_call_target="tpu_custom_call" | custom-call | tf_op jit(solution)/shard_map/pallas_call | solution.py:230
  37.3 2.2 %collective-permute-start.8 = (bf16[16,896]{1,0:T(8,128)(2,1)S(1)}, bf16[16,896]{1,0:T(8,128)(2,1)S(1)}, u32[]{:S(2)}, u32[]{:S(2)}) collective-permute-start(bf16[16,896]{1,0:T(8,128)(2,1)S(1)} %get-tuple-element.22), channel_id=1, source_target_pairs={{0,12},{4,0},{8,4},{12,8},{1,13},{5,1},{9,5},{13,9},{2,14},{6,2},{... | collective-permute-start | bytes 86024 | tf_op jit(solution)/shard_map/ppermute | solution.py:240
  39.5 1.1 %collective-permute-start.9 = (bf16[16,896]{1,0:T(8,128)(2,1)S(1)}, bf16[16,896]{1,0:T(8,128)(2,1)S(1)}, u32[]{:S(2)}, u32[]{:S(2)}) collective-permute-start(bf16[16,896]{1,0:T(8,128)(2,1)S(1)} %get-tuple-element.23), channel_id=1, source_target_pairs={{0,8},{4,12},{8,0},{12,4},{1,9},{5,13},{9,1},{13,5},{2,10},{6,14},... | collective-permute-start | bytes 86024 | tf_op jit(solution)/shard_map/ppermute | solution.py:240
  40.6 0.0 collective-permute-start.10
  40.6 0.6 %collective-permute-done.8 = bf16[16,896]{1,0:T(8,128)(2,1)S(1)} collective-permute-done((bf16[16,896]{1,0:T(8,128)(2,1)S(1)}, bf16[16,896]{1,0:T(8,128)(2,1)S(1)}, u32[]{:S(2)}, u32[]{:S(2)}) %collective-permute-start.8) | collective-permute-done | bytes 28704 | tf_op jit(solution)/shard_map/ppermute | solution.py:240
  41.2 3.0 %collective-permute-done.9 = bf16[16,896]{1,0:T(8,128)(2,1)S(1)} collective-permute-done((bf16[16,896]{1,0:T(8,128)(2,1)S(1)}, bf16[16,896]{1,0:T(8,128)(2,1)S(1)}, u32[]{:S(2)}, u32[]{:S(2)}) %collective-permute-start.9) | collective-permute-done | bytes 28704 | tf_op jit(solution)/shard_map/ppermute | solution.py:240
  44.2 2.0 %collective-permute-done.10 = bf16[16,896]{1,0:T(8,128)(2,1)S(1)} collective-permute-done((bf16[16,896]{1,0:T(8,128)(2,1)S(1)}, bf16[16,896]{1,0:T(8,128)(2,1)S(1)}, u32[]{:S(2)}, u32[]{:S(2)}) %collective-permute-start.10) | collective-permute-done | bytes 28704 | tf_op jit(solution)/shard_map/ppermute | solution.py:240
  46.3 0.6 %add_convert_fusion = bf16[16,896]{1,0:T(8,128)(2,1)} fusion(bf16[16,896]{1,0:T(8,128)(2,1)S(1)} %collective-permute-done.10, bf16[16,896]{1,0:T(8,128)(2,1)S(1)} %collective-permute-done.9, f32[16,896]{1,0:T(8,128)S(1)} %get-tuple-element.21, bf16[16,896]{1,0:T(8,128)(2,1)S(1)} %collective-permute-done.8), kind=kLoop, calls=%fused_computation | loop fusion | flops 100352 | bytes 172032 | tf_op jit(solution)/shard_map/convert_element_type | solution.py:242
  (1 shorter events, 0.0 us)
Async XLA Ops:
  3.8 10.9 %copy-start = (bf16[1,896,16]{1,2,0:T(8,128)(2,1)S(1)}, bf16[1,896,16]{1,2,0:T(8,128)(2,1)}, u32[]{:S(2)}) copy-start(bf16[1,896,16]{1,2,0:T(8,128)(2,1)} %param.10) | copy-start | bytes 86020
  3.8 10.1 %collective-permute-start.2 = (bf16[16,1024]{1,0:T(8,128)(2,1)S(1)}, bf16[16,1024]{1,0:T(8,128)(2,1)S(1)}, u32[]{:S(2)}, u32[]{:S(2)}) collective-permute-start(bf16[16,1024]{1,0:T(8,128)(2,1)S(1)} %get-tuple-element.15.refs_0_.refs_4_), channel_id=1, source_target_pairs={{0,12},{4,0},{8,4},{12,8},{1,13},{5,1},{9,5},{13,9},{2,14},{6,2},{... | collective-permute-start | bytes 98312 | tf_op jit(solution)/shard_map/ppermute | solution.py:192
  9.0 5.0 %collective-permute-start.1 = (bf16[16,1024]{1,0:T(8,128)(2,1)S(1)}, bf16[16,1024]{1,0:T(8,128)(2,1)S(1)}, u32[]{:S(2)}, u32[]{:S(2)}) collective-permute-start(bf16[16,1024]{1,0:T(8,128)(2,1)S(1)} %get-tuple-element.15.refs_0_.refs_4_), channel_id=1, source_target_pairs={{0,8},{4,12},{8,0},{12,4},{1,9},{5,13},{9,1},{13,5},{2,10},{6,14},... | collective-permute-start | bytes 98312 | tf_op jit(solution)/shard_map/ppermute | solution.py:192
  9.0 5.7 %collective-permute-start = (bf16[16,1024]{1,0:T(8,128)(2,1)S(1)}, bf16[16,1024]{1,0:T(8,128)(2,1)S(1)}, u32[]{:S(2)}, u32[]{:S(2)}) collective-permute-start(bf16[16,1024]{1,0:T(8,128)(2,1)S(1)} %get-tuple-element.15.refs_0_.refs_4_), channel_id=1, source_target_pairs={{0,4},{4,8},{8,12},{12,0},{1,5},{5,9},{9,13},{13,1},{2,6},{6,10},{... | collective-permute-start | bytes 98312 | tf_op jit(solution)/shard_map/ppermute | solution.py:192
  14.7 21.1 %slice-start = ((s8[8486912]{0:T(1024)(128)(4,1)}), s8[4194304]{0:T(1024)(128)(4,1)S(1)}, s32[]{:S(2)}) async-start(s8[8486912]{0:T(1024)(128)(4,1)} %bitcast.6), calls=%async_computation | async-start | bytes 8388608
  14.7 21.1 %slice-start.1 = ((s8[8486912]{0:T(1024)(128)(4,1)}), s8[4194304]{0:T(1024)(128)(4,1)S(1)}, s32[]{:S(2)}) async-start(s8[8486912]{0:T(1024)(128)(4,1)} %bitcast.6), calls=%async_computation.1 | async-start | bytes 8388608
  14.7 21.1 %slice-start.2 = ((s8[8486912]{0:T(1024)(128)(4,1)}), s8[98304]{0:T(1024)(128)(4,1)S(1)}, s32[]{:S(2)}) async-start(s8[8486912]{0:T(1024)(128)(4,1)} %bitcast.6), calls=%async_computation.2 | async-start | bytes 196608
  14.7 21.1 %copy-start.1 = (bf16[1,16,896]{2,1,0:T(8,128)(2,1)S(1)}, bf16[1,16,896]{2,1,0:T(8,128)(2,1)}, u32[]{:S(2)}) copy-start(bf16[1,16,896]{2,1,0:T(8,128)(2,1)} %param.11) | copy-start | bytes 86020
  17.4 2.1 %collective-permute-start.3 = (bf16[32,9600]{1,0:T(8,128)(2,1)S(1)}, bf16[32,9600]{1,0:T(8,128)(2,1)S(1)}, u32[]{:S(2)}, u32[]{:S(2)}) collective-permute-start(bf16[32,9600]{1,0:T(8,128)(2,1)S(1)} %get-tuple-element.18), channel_id=1, source_target_pairs={{0,1},{1,0},{2,3},{3,2},{4,5},{5,4},{6,7},{7,6},{8,9},{9,8},{10,11... | collective-permute-start | bytes 1843208 | tf_op jit(solution)/shard_map/ppermute | solution.py:167
  19.6 9.4 %collective-permute-start.4 = (bf16[16,9600]{1,0:T(8,128)(2,1)S(1)}, bf16[16,9600]{1,0:T(8,128)(2,1)S(1)}, u32[]{:S(2)}, u32[]{:S(2)}) collective-permute-start(bf16[16,9600]{1,0:T(8,128)(2,1)S(1)} %get-tuple-element.20), channel_id=1, source_target_pairs={{0,2},{1,3},{2,0},{3,1},{4,6},{5,7},{6,4},{7,5},{8,10},{9,11},{10,... | collective-permute-start | bytes 921608 | tf_op jit(solution)/shard_map/ppermute | solution.py:167
  29.1 5.3 %collective-permute-start.5 = (bf16[16,4864]{1,0:T(8,128)(2,1)S(1)}, bf16[16,4864]{1,0:T(8,128)(2,1)S(1)}, u32[]{:S(2)}, u32[]{:S(2)}) collective-permute-start(bf16[16,4864]{1,0:T(8,128)(2,1)S(1)} %shard_map.77.refs_0_), channel_id=1, source_target_pairs={{0,2},{1,3},{2,0},{3,1},{4,6},{5,7},{6,4},{7,5},{8,10},{9,11},{10,... | collective-permute-start | bytes 466952 | tf_op jit(solution)/shard_map/ppermute | solution.py:167
  30.6 3.7 %collective-permute-start.6 = (bf16[16,4864]{1,0:T(8,128)(2,1)S(1)}, bf16[16,4864]{1,0:T(8,128)(2,1)S(1)}, u32[]{:S(2)}, u32[]{:S(2)}) collective-permute-start(bf16[16,4864]{1,0:T(8,128)(2,1)S(1)} %shard_map.77.refs_0_), channel_id=1, source_target_pairs={{0,1},{1,0},{2,3},{3,2},{4,5},{5,4},{6,7},{7,6},{8,9},{9,8},{10,11... | collective-permute-start | bytes 466952 | tf_op jit(solution)/shard_map/ppermute | solution.py:167
  34.4 1.4 %collective-permute-start.7 = (bf16[16,4864]{1,0:T(8,128)(2,1)S(1)}, bf16[16,4864]{1,0:T(8,128)(2,1)S(1)}, u32[]{:S(2)}, u32[]{:S(2)}) collective-permute-start(bf16[16,4864]{1,0:T(8,128)(2,1)S(1)} %collective-permute-done.5.refs_1_), channel_id=1, source_target_pairs={{0,1},{1,0},{2,3},{3,2},{4,5},{5,4},{6,7},{7,6},{8,9},{9,8},{10,11... | collective-permute-start | bytes 466952 | tf_op jit(solution)/shard_map/ppermute | solution.py:167
  37.3 3.9 %collective-permute-start.8 = (bf16[16,896]{1,0:T(8,128)(2,1)S(1)}, bf16[16,896]{1,0:T(8,128)(2,1)S(1)}, u32[]{:S(2)}, u32[]{:S(2)}) collective-permute-start(bf16[16,896]{1,0:T(8,128)(2,1)S(1)} %get-tuple-element.22), channel_id=1, source_target_pairs={{0,12},{4,0},{8,4},{12,8},{1,13},{5,1},{9,5},{13,9},{2,14},{6,2},{... | collective-permute-start | bytes 86024 | tf_op jit(solution)/shard_map/ppermute | solution.py:240
  39.5 4.8 %collective-permute-start.9 = (bf16[16,896]{1,0:T(8,128)(2,1)S(1)}, bf16[16,896]{1,0:T(8,128)(2,1)S(1)}, u32[]{:S(2)}, u32[]{:S(2)}) collective-permute-start(bf16[16,896]{1,0:T(8,128)(2,1)S(1)} %get-tuple-element.23), channel_id=1, source_target_pairs={{0,8},{4,12},{8,0},{12,4},{1,9},{5,13},{9,1},{13,5},{2,10},{6,14},... | collective-permute-start | bytes 86024 | tf_op jit(solution)/shard_map/ppermute | solution.py:240
  40.6 5.7 %collective-permute-start.10 = (bf16[16,896]{1,0:T(8,128)(2,1)S(1)}, bf16[16,896]{1,0:T(8,128)(2,1)S(1)}, u32[]{:S(2)}, u32[]{:S(2)}) collective-permute-start(bf16[16,896]{1,0:T(8,128)(2,1)S(1)} %get-tuple-element.24), channel_id=1, source_target_pairs={{0,4},{4,8},{8,12},{12,0},{1,5},{5,9},{9,13},{13,1},{2,6},{6,10},{... | collective-permute-start | bytes 86024 | tf_op jit(solution)/shard_map/ppermute | solution.py:240
